TPU v7x, 512 devices: a 8x2x16 block of a 8x8x16 slice. The times are simulated.
512 devices in a mesh: groups: 2 (over y), tensor: 32 (over z, core), section: 8 (over x).
Axes of the slice: x: 8, y: 2, z: 16, core: 2. Of those that a mesh axis runs over, the one named last changes fastest.
The devices are a block of a 8x8x16 slice.
Arguments:
- hidden: bfloat16 [128, 8192], P('groups', 'tensor'), parts along dimension 0, may hold values from -6 to 6
- norm_gain: bfloat16 [8, 8192], P('section'), may hold values from 0.5 to 1.5
- query_weight: bfloat16 [8, 8192, 4096], P('section', None, 'tensor'), may hold values from -0.0625 to 0.0625
- query_bias: bfloat16 [8, 4096], P('section', 'tensor'), may hold values from -10 to 10
- kv_weight: bfloat16 [8, 8192, 1024], P('section', None, 'tensor'), may hold values from -0.0625 to 0.0625
- out_weight: bfloat16 [8, 4096, 8192], P('section', None, 'tensor'), may hold values from -0.09375 to 0.09375
- kv_pool: bfloat16 [8, 384, 16, 1024], P('section', ('groups', 'tensor')), parts along dimension 1, may hold values from -8 to 8
- page_table: int32 [128, 4], P(('groups', 'tensor')), parts along dimension 0, may hold values from 0 to 191, as said below
- context_len: int32 [128], P(('groups', 'tensor')), parts along dimension 0, may hold values from 33 to 64, as said below
Outputs:
- result: bfloat16 [128, 8192], P(('groups', 'section'), 'tensor'), parts along dimension 0
There are 2 independent parts, one for each index of `groups`. A program takes and returns all parts, laid end to end along the dimension named above; an argument that names none is the same for every part. Nothing has to cross between parts.
Inputs may be any that keep to these rules, and one draw needn't show every extreme that they name: `page_table`: sample r belongs to block k = r // 2; its 4 pages lie in k * 6 to (k + 1) * 6 - 1. The first 2 pages are the same for all samples of a block, every other page belongs to one sample only. `context_len`: some sample has 64 cached tokens.
All inputs are finite; a program needn't handle non-finite values.
Results may differ from a plain program's by a relative error of at most 0.018.
Values may be sent and summed in bfloat16 or wider, within the bound.
A program may use at most 64 MiB of HBM per device.

v0:
```python
import jax
import jax.numpy as jnp
from jax import lax
from jax.sharding import Mesh
from jax.sharding import PartitionSpec as P

HD = 128
KVH = 4
TENSOR = ("tensor_0", "tensor_1")
GROUPS_TENSOR = ("groups", "tensor_0", "tensor_1")
epsilon = 1e-06
rope_base = 1000000.0


def laid_out(tiles, dim):
    lengths = list(tiles.shape[1:])
    lengths[dim] *= tiles.shape[0]
    return jnp.moveaxis(tiles, 0, dim).reshape(lengths)


def all_blocks(shard, axes, turns):
    tiles = shard[None]
    for k in turns:
        tiles = lax.all_gather(tiles, axes[k], axis=0, tiled=True)
    block = [lax.axis_size(axes[k]) for k in reversed(turns)]
    tiles = tiles.reshape(*block, *shard.shape)
    turned = sorted(range(len(turns)), key=lambda place: turns[len(turns) - 1 - place])
    return tiles.transpose(*turned, *range(len(turns), tiles.ndim)).reshape(-1, *shard.shape)


def gathered_by_axis(shard, axes, turns, dim):
    return laid_out(all_blocks(shard, axes, turns), dim)


def shifted(value, axis, steps):
    count = lax.axis_size(axis)
    initial, last = (max(0, -steps), min(count, count - steps))
    return lax.ppermute(value, axis, [(source, source + steps) for source in range(initial, last)])


def rotate(values, position):
    head_size = values.shape[-1]
    half_size = head_size // 2
    frequency = rope_base ** (-(jnp.arange(half_size, dtype=jnp.float32) * 2.0) / head_size)
    angles = position.astype(jnp.float32)[:, None] * frequency[None, :]
    cosine = jnp.cos(angles)[:, None, :]
    sine_part = jnp.sin(angles)[:, None, :]
    front_half = values[..., :half_size]
    back_half = values[..., half_size:]
    return jnp.concatenate(
        [front_half * cosine - back_half * sine_part, back_half * cosine + front_half * sine_part],
        axis=-1,
    )


def attend(queries, key_new, value_new, cached, position):
    row_count, head_count, head_size = queries.shape
    kv_heads = key_new.shape[1]
    group_size = head_count // kv_heads
    span_len = cached.shape[1]
    keys_all = cached[:, :, : kv_heads * head_size].reshape(
        row_count, span_len, kv_heads, head_size
    )
    values_all = cached[:, :, kv_heads * head_size :].reshape(
        row_count, span_len, kv_heads, head_size
    )
    grouped = queries.reshape(row_count, kv_heads, group_size, head_size)
    scaling = head_size ** (-0.5)
    scores = (
        jnp.einsum("rkgd,rskd->rkgs", grouped, keys_all, preferred_element_type=jnp.float32)
        * scaling
    )
    own_score = (
        jnp.einsum("rkgd,rkd->rkg", grouped, key_new, preferred_element_type=jnp.float32) * scaling
    )
    usable = (jnp.arange(span_len, dtype=jnp.int32)[None, :] < position[:, None])[:, None, None, :]
    row_max = jnp.maximum(jnp.max(jnp.where(usable, scores, -1e30), axis=-1), own_score)
    weights = jnp.where(usable, jnp.exp(scores - row_max[..., None]), 0.0)
    own_weight = jnp.exp(own_score - row_max)
    denominator = jnp.sum(weights, axis=-1) + own_weight
    weights = (weights / denominator[..., None]).astype(jnp.bfloat16)
    own_weight = (own_weight / denominator).astype(jnp.bfloat16)
    mixture = jnp.einsum("rkgs,rskd->rkgd", weights, values_all, preferred_element_type=jnp.float32)
    mixture = (
        mixture
        + own_weight.astype(jnp.float32)[..., None] * value_new.astype(jnp.float32)[:, :, None, :]
    )
    return mixture.reshape(row_count, head_count * head_size).astype(jnp.bfloat16)


def shards(
    hidden,
    norm_gain,
    query_weight,
    query_bias,
    kv_weight,
    out_weight,
    kv_pool,
    page_table,
    context_len,
):
    slot_count = lax.axis_size(TENSOR)
    section_count = lax.axis_size("section")
    section_id = lax.axis_index("section")
    tensor_id = lax.axis_index(TENSOR)
    row_total, width_dev = hidden.shape
    row_dev = row_total // slot_count
    pool_pages = kv_pool.shape[1]
    gain_row = norm_gain[0].astype(jnp.float32)
    query_proj = query_weight[0]
    bias_row = query_bias[0].astype(jnp.float32)
    kv_proj = kv_weight[0]
    out_proj = out_weight[0]
    pool_layer = kv_pool[0]
    local_pages = page_table - tensor_id * pool_pages
    per_piece = row_dev // row_dev
    tick_count = section_count + row_dev - 1
    is_first = section_id == 0
    finished = [None] * row_dev
    carried = jnp.zeros((slot_count * per_piece, width_dev), jnp.bfloat16)
    for tick_index in range(tick_count):
        if tick_index < row_dev:
            blocks = hidden.reshape(slot_count, row_dev, hidden.shape[1])
            chosen = blocks[:, tick_index * per_piece : (tick_index + 1) * per_piece]
            carried = jnp.where(
                is_first, chosen.reshape(slot_count * per_piece, hidden.shape[1]), carried
            )
        whole = gathered_by_axis(carried, TENSOR, (0, 1), 1)
        wide_rows = whole.astype(jnp.float32)
        mean_sq = jnp.mean(wide_rows * wide_rows, axis=1, keepdims=True)
        normed = (wide_rows * lax.rsqrt(mean_sq + epsilon) * gain_row).astype(jnp.bfloat16)
        queries = (
            jnp.dot(normed, query_proj, preferred_element_type=jnp.float32) + bias_row
        ).astype(jnp.bfloat16)
        fresh_kv = jnp.dot(normed, kv_proj, preferred_element_type=jnp.float32).astype(jnp.bfloat16)
        query_rows = lax.all_to_all(queries, TENSOR, split_axis=0, concat_axis=1, tiled=True)
        fresh_rows = lax.all_to_all(fresh_kv, TENSOR, split_axis=0, concat_axis=1, tiled=True)
        piece_index = jnp.clip(tick_index - section_id, 0, row_dev - 1)
        start_row = piece_index * per_piece
        position = lax.dynamic_slice_in_dim(context_len, start_row, per_piece, 0)
        page_ids = lax.dynamic_slice_in_dim(local_pages, start_row, per_piece, 0)
        cached = pool_layer[page_ids].reshape(per_piece, -1, pool_layer.shape[-1])
        rotated = rotate(
            query_rows.reshape(per_piece, -1, HD).astype(jnp.float32), position
        ).astype(jnp.bfloat16)
        key_new = rotate(
            fresh_rows[:, : KVH * HD].reshape(per_piece, KVH, HD).astype(jnp.float32), position
        ).astype(jnp.bfloat16)
        value_new = fresh_rows[:, KVH * HD :].reshape(per_piece, KVH, HD)
        mixture = attend(rotated, key_new, value_new, cached, position)
        carried = (
            carried.astype(jnp.float32)
            + jnp.dot(
                lax.all_gather(mixture, TENSOR, axis=0, tiled=True),
                out_proj,
                preferred_element_type=jnp.float32,
            )
        ).astype(jnp.bfloat16)
        if tick_index >= section_count - 1:
            finished[tick_index - section_count + 1] = carried
        if tick_index < tick_count - 1:
            carried = shifted(carried, "section", 1)
    stacked = jnp.concatenate(
        [done_part.reshape(slot_count, per_piece, width_dev) for done_part in finished], axis=1
    )
    result = stacked.reshape(row_total, width_dev)
    is_last = section_id == section_count - 1
    outgoing = jnp.where(is_last, result, jnp.zeros_like(result))[None]
    spread = lax.all_to_all(outgoing, "section", split_axis=1, concat_axis=0, tiled=True)
    return spread[section_count - 1]


def solution(mesh):
    finer = Mesh(
        mesh.devices.reshape(mesh.shape["groups"], 16, 2, mesh.shape["section"]),
        ("groups", "tensor_0", "tensor_1", "section"),
    )
    in_specs = (
        P("groups", TENSOR),
        P("section", None),
        P("section", None, TENSOR),
        P("section", TENSOR),
        P("section", None, TENSOR),
        P("section", None, TENSOR),
        P("section", GROUPS_TENSOR, None, None),
        P(GROUPS_TENSOR, None),
        P(GROUPS_TENSOR),
    )
    out_specs = P(("groups", "section"), TENSOR)
    return jax.shard_map(
        shards, mesh=finer, in_specs=in_specs, out_specs=out_specs, check_vma=False
    )
```

profile of v0, /device:TPU:80, one launch (start us, length us, event | category | flops | bytes accessed | tf_op | source)
XLA Modules:
  0.0 1020.4 jit_solution(11074019601654187876)
XLA Ops:
  1.0 69.5 %all-gather = bf16[512,1,256]{2,0,1:T(8,128)(2,1)S(1)} all-gather(bf16[32,1,256]{2,0,1:T(8,128)(2,1)S(1)} %copy_select_fusion), channel_id=2, replica_groups=mesh['groups'=2,'tensor_0'=16,'tensor_1'=2,'section'=8] {'tensor_0'}, dimensions={0}, use_global_device_ids=true | all-gather | bytes 278528 | tf_op jit(solution)/shard_map/all_gather | solution.py:24
  116.3 12.4 %all-to-all-start = ((bf16[32,1,128]{2,1,0:T(2,128)(2,1)}), bf16[32,1,128]{2,1,0:T(2,128)(2,1)S(1)}, u32[]{:S(2)}, u32[]{:S(2)}) async-start(bf16[32,1,128]{2,1,0:T(2,128)(2,1)} %copy.159), calls=%async_computation | async-start | bytes 32768 | tf_op jit(solution)/shard_map/all_to_all | solution.py:136
  129.7 10.8 %all-to-all-done = bf16[32,1,128]{2,1,0:T(2,128)(2,1)S(1)} async-done(((bf16[32,1,128]{2,1,0:T(2,128)(2,1)}), bf16[32,1,128]{2,1,0:T(2,128)(2,1)S(1)}, u32[]{:S(2)}, u32[]{:S(2)}) %all-to-all-start) | async-done | bytes 8224 | tf_op jit(solution)/shard_map/all_to_all | solution.py:136
  141.5 28.8 %all-gather.9 = bf16[32,1,4096]{2,1,0:T(2,128)(2,1)S(1)} all-gather(bf16[1,1,4096]{2,1,0:T(2,128)(2,1)S(1)} %reshape.2331), channel_id=1, replica_groups=mesh['groups'=2,'tensor_0'=16,'tensor_1'=2,'section'=8] {'tensor_0','ten..., dimensions={0}, use_global_device_ids=true | all-gather | bytes 270336 | tf_op jit(solution)/shard_map/all_gather | solution.py:154
  175.8 28.8 %all-gather.1 = bf16[512,256]{1,0:T(8,128)(2,1)S(1)} all-gather(bf16[32,256]{1,0:T(8,128)(2,1)S(1)} %fusion.214), channel_id=3, replica_groups=mesh['groups'=2,'tensor_0'=16,'tensor_1'=2,'section'=8] {'tensor_0'}, dimensions={0}, use_global_device_ids=true | all-gather | bytes 278528 | tf_op jit(solution)/shard_map/all_gather | solution.py:24
  208.4 5.6 all-to-all-start.3
  216.7 9.1 all-to-all-done.3
  230.8 11.4 %all-to-all-done.2 = bf16[32,1,128]{2,1,0:T(2,128)(2,1)S(1)} async-done(((bf16[32,1,128]{2,1,0:T(2,128)(2,1)}), bf16[32,1,128]{2,1,0:T(2,128)(2,1)S(1)}, u32[]{:S(2)}, u32[]{:S(2)}) %all-to-all-start.2) | async-done | bytes 8224 | tf_op jit(solution)/shard_map/all_to_all | solution.py:136
  243.3 28.8 %all-gather.10 = bf16[32,1,4096]{2,1,0:T(2,128)(2,1)S(1)} all-gather(bf16[1,1,4096]{2,1,0:T(2,128)(2,1)S(1)} %reshape.2333), channel_id=1, replica_groups=mesh['groups'=2,'tensor_0'=16,'tensor_1'=2,'section'=8] {'tensor_0','ten..., dimensions={0}, use_global_device_ids=true | all-gather | bytes 270336 | tf_op jit(solution)/shard_map/all_gather | solution.py:154
  278.3 29.3 %all-gather.2 = bf16[512,256]{1,0:T(8,128)(2,1)S(1)} all-gather(bf16[32,256]{1,0:T(8,128)(2,1)S(1)} %collective-permute-done.1), channel_id=4, replica_groups=mesh['groups'=2,'tensor_0'=16,'tensor_1'=2,'section'=8] {'tensor_0'}, dimensions={0}, use_global_device_ids=true | all-gather | bytes 278528 | tf_op jit(solution)/shard_map/all_gather | solution.py:24
  311.4 5.7 all-to-all-start.5
  319.8 9.1 all-to-all-done.5
  333.9 11.4 %all-to-all-done.4 = bf16[32,1,128]{2,1,0:T(2,128)(2,1)S(1)} async-done(((bf16[32,1,128]{2,1,0:T(2,128)(2,1)}), bf16[32,1,128]{2,1,0:T(2,128)(2,1)S(1)}, u32[]{:S(2)}, u32[]{:S(2)}) %all-to-all-start.4) | async-done | bytes 8224 | tf_op jit(solution)/shard_map/all_to_all | solution.py:136
  346.4 28.9 %all-gather.11 = bf16[32,1,4096]{2,1,0:T(2,128)(2,1)S(1)} all-gather(bf16[1,1,4096]{2,1,0:T(2,128)(2,1)S(1)} %reshape.2335), channel_id=1, replica_groups=mesh['groups'=2,'tensor_0'=16,'tensor_1'=2,'section'=8] {'tensor_0','ten..., dimensions={0}, use_global_device_ids=true | all-gather | bytes 270336 | tf_op jit(solution)/shard_map/all_gather | solution.py:154
  381.6 28.7 %all-gather.3 = bf16[512,256]{1,0:T(8,128)(2,1)S(1)} all-gather(bf16[32,256]{1,0:T(8,128)(2,1)S(1)} %collective-permute-done.2), channel_id=5, replica_groups=mesh['groups'=2,'tensor_0'=16,'tensor_1'=2,'section'=8] {'tensor_0'}, dimensions={0}, use_global_device_ids=true | all-gather | bytes 278528 | tf_op jit(solution)/shard_map/all_gather | solution.py:24
  414.1 5.7 all-to-all-start.7
  422.5 9.1 all-to-all-done.7
  436.6 11.4 %all-to-all-done.6 = bf16[32,1,128]{2,1,0:T(2,128)(2,1)S(1)} async-done(((bf16[32,1,128]{2,1,0:T(2,128)(2,1)}), bf16[32,1,128]{2,1,0:T(2,128)(2,1)S(1)}, u32[]{:S(2)}, u32[]{:S(2)}) %all-to-all-start.6) | async-done | bytes 8224 | tf_op jit(solution)/shard_map/all_to_all | solution.py:136
  449.0 28.8 %all-gather.12 = bf16[32,1,4096]{2,1,0:T(2,128)(2,1)S(1)} all-gather(bf16[1,1,4096]{2,1,0:T(2,128)(2,1)S(1)} %reshape.2337), channel_id=1, replica_groups=mesh['groups'=2,'tensor_0'=16,'tensor_1'=2,'section'=8] {'tensor_0','ten..., dimensions={0}, use_global_device_ids=true | all-gather | bytes 270336 | tf_op jit(solution)/shard_map/all_gather | solution.py:154
  484.1 28.8 %all-gather.4 = bf16[512,256]{1,0:T(8,128)(2,1)S(1)} all-gather(bf16[32,256]{1,0:T(8,128)(2,1)S(1)} %collective-permute-done.3), channel_id=6, replica_groups=mesh['groups'=2,'tensor_0'=16,'tensor_1'=2,'section'=8] {'tensor_0'}, dimensions={0}, use_global_device_ids=true | all-gather | bytes 278528 | tf_op jit(solution)/shard_map/all_gather | solution.py:24
  516.8 5.8 all-to-all-start.9
  525.3 9.5 all-to-all-done.9
  539.8 11.4 %all-to-all-done.8 = bf16[32,1,128]{2,1,0:T(2,128)(2,1)S(1)} async-done(((bf16[32,1,128]{2,1,0:T(2,128)(2,1)}), bf16[32,1,128]{2,1,0:T(2,128)(2,1)S(1)}, u32[]{:S(2)}, u32[]{:S(2)}) %all-to-all-start.8) | async-done | bytes 8224 | tf_op jit(solution)/shard_map/all_to_all | solution.py:136
  552.2 28.8 %all-gather.13 = bf16[32,1,4096]{2,1,0:T(2,128)(2,1)S(1)} all-gather(bf16[1,1,4096]{2,1,0:T(2,128)(2,1)S(1)} %reshape.2339), channel_id=1, replica_groups=mesh['groups'=2,'tensor_0'=16,'tensor_1'=2,'section'=8] {'tensor_0','ten..., dimensions={0}, use_global_device_ids=true | all-gather | bytes 270336 | tf_op jit(solution)/shard_map/all_gather | solution.py:154
  587.3 28.8 %all-gather.5 = bf16[512,256]{1,0:T(8,128)(2,1)S(1)} all-gather(bf16[32,256]{1,0:T(8,128)(2,1)S(1)} %collective-permute-done.4), channel_id=7, replica_groups=mesh['groups'=2,'tensor_0'=16,'tensor_1'=2,'section'=8] {'tensor_0'}, dimensions={0}, use_global_device_ids=true | all-gather | bytes 278528 | tf_op jit(solution)/shard_map/all_gather | solution.py:24
  619.9 5.7 all-to-all-start.11
  628.3 9.1 all-to-all-done.11
  642.5 11.4 %all-to-all-done.10 = bf16[32,1,128]{2,1,0:T(2,128)(2,1)S(1)} async-done(((bf16[32,1,128]{2,1,0:T(2,128)(2,1)}), bf16[32,1,128]{2,1,0:T(2,128)(2,1)S(1)}, u32[]{:S(2)}, u32[]{:S(2)}) %all-to-all-start.10) | async-done | bytes 8224 | tf_op jit(solution)/shard_map/all_to_all | solution.py:136
  654.9 28.9 %all-gather.14 = bf16[32,1,4096]{2,1,0:T(2,128)(2,1)S(1)} all-gather(bf16[1,1,4096]{2,1,0:T(2,128)(2,1)S(1)} %reshape.2341), channel_id=1, replica_groups=mesh['groups'=2,'tensor_0'=16,'tensor_1'=2,'section'=8] {'tensor_0','ten..., dimensions={0}, use_global_device_ids=true | all-gather | bytes 270336 | tf_op jit(solution)/shard_map/all_gather | solution.py:154
  684.3 5.6 collective-permute-start.5
  691.3 28.7 %all-gather.6 = bf16[512,256]{1,0:T(8,128)(2,1)S(1)} all-gather(bf16[32,256]{1,0:T(8,128)(2,1)S(1)} %collective-permute-done.5), channel_id=8, replica_groups=mesh['groups'=2,'tensor_0'=16,'tensor_1'=2,'section'=8] {'tensor_0'}, dimensions={0}, use_global_device_ids=true | all-gather | bytes 278528 | tf_op jit(solution)/shard_map/all_gather | solution.py:24
  723.8 5.7 all-to-all-start.13
  732.2 9.1 all-to-all-done.13
  746.3 11.4 %all-to-all-done.12 = bf16[32,1,128]{2,1,0:T(2,128)(2,1)S(1)} async-done(((bf16[32,1,128]{2,1,0:T(2,128)(2,1)}), bf16[32,1,128]{2,1,0:T(2,128)(2,1)S(1)}, u32[]{:S(2)}, u32[]{:S(2)}) %all-to-all-start.12) | async-done | bytes 8224 | tf_op jit(solution)/shard_map/all_to_all | solution.py:136
  758.8 29.1 %all-gather.15 = bf16[32,1,4096]{2,1,0:T(2,128)(2,1)S(1)} all-gather(bf16[1,1,4096]{2,1,0:T(2,128)(2,1)S(1)} %reshape.2343), channel_id=1, replica_groups=mesh['groups'=2,'tensor_0'=16,'tensor_1'=2,'section'=8] {'tensor_0','ten..., dimensions={0}, use_global_device_ids=true | all-gather | bytes 270336 | tf_op jit(solution)/shard_map/all_gather | solution.py:154
  788.4 5.6 collective-permute-start.6
  795.4 28.7 %all-gather.7 = bf16[512,256]{1,0:T(8,128)(2,1)S(1)} all-gather(bf16[32,256]{1,0:T(8,128)(2,1)S(1)} %collective-permute-done.6), channel_id=9, replica_groups=mesh['groups'=2,'tensor_0'=16,'tensor_1'=2,'section'=8] {'tensor_0'}, dimensions={0}, use_global_device_ids=true | all-gather | bytes 278528 | tf_op jit(solution)/shard_map/all_gather | solution.py:24
  827.9 5.7 all-to-all-start.15
  836.3 9.1 all-to-all-done.15
  850.4 11.4 %all-to-all-done.14 = bf16[32,1,128]{2,1,0:T(2,128)(2,1)S(1)} async-done(((bf16[32,1,128]{2,1,0:T(2,128)(2,1)}), bf16[32,1,128]{2,1,0:T(2,128)(2,1)S(1)}, u32[]{:S(2)}, u32[]{:S(2)}) %all-to-all-start.14) | async-done | bytes 8224 | tf_op jit(solution)/shard_map/all_to_all | solution.py:136
  862.8 28.8 %all-gather.16 = bf16[32,1,4096]{2,1,0:T(2,128)(2,1)S(1)} all-gather(bf16[1,1,4096]{2,1,0:T(2,128)(2,1)S(1)} %reshape.2345), channel_id=1, replica_groups=mesh['groups'=2,'tensor_0'=16,'tensor_1'=2,'section'=8] {'tensor_0','ten..., dimensions={0}, use_global_device_ids=true | all-gather | bytes 270336 | tf_op jit(solution)/shard_map/all_gather | solution.py:154
  892.1 5.6 collective-permute-start.7
  899.1 28.8 %all-gather.8 = bf16[512,256]{1,0:T(8,128)(2,1)S(1)} all-gather(bf16[32,256]{1,0:T(8,128)(2,1)S(1)} %collective-permute-done.7), channel_id=10, replica_groups=mesh['groups'=2,'tensor_0'=16,'tensor_1'=2,'section'=8] {'tensor_0'}, dimensions={0}, use_global_device_ids=true | all-gather | bytes 278528 | tf_op jit(solution)/shard_map/all_gather | solution.py:24
  931.7 5.7 all-to-all-start.17
  940.1 9.1 all-to-all-done.17
  954.3 11.4 %all-to-all-done.16 = bf16[32,1,128]{2,1,0:T(2,128)(2,1)S(1)} async-done(((bf16[32,1,128]{2,1,0:T(2,128)(2,1)}), bf16[32,1,128]{2,1,0:T(2,128)(2,1)S(1)}, u32[]{:S(2)}, u32[]{:S(2)}) %all-to-all-start.16) | async-done | bytes 8224 | tf_op jit(solution)/shard_map/all_to_all | solution.py:136
  966.7 28.9 %all-gather.17 = bf16[32,1,4096]{2,1,0:T(2,128)(2,1)S(1)} all-gather(bf16[1,1,4096]{2,1,0:T(2,128)(2,1)S(1)} %reshape.2347), channel_id=1, replica_groups=mesh['groups'=2,'tensor_0'=16,'tensor_1'=2,'section'=8] {'tensor_0','ten..., dimensions={0}, use_global_device_ids=true | all-gather | bytes 270336 | tf_op jit(solution)/shard_map/all_gather | solution.py:154
  997.6 22.0 %all_to_all.273 = bf16[8,2,1024]{2,1,0:T(2,128)(2,1)S(1)} all-to-all(bf16[8,2,1024]{2,1,0:T(2,128)(2,1)S(1)} %reshape.2392), channel_id=1, replica_groups=mesh['groups'=2,'tensor_0'=16,'tensor_1'=2,'section'=8] {'section'}, dimensions={0} | all-to-all | bytes 65536 | tf_op jit(solution)/shard_map/all_to_all | solution.py:169
  (425 shorter events, 181.0 us)
Async XLA Ops:
  0.0 170.2 %copy-start = (bf16[1,4096,256]{2,1,0:T(8,128)(2,1)S(1)}, bf16[1,4096,256]{2,1,0:T(8,128)(2,1)}, u32[]{:S(2)}) copy-start(bf16[1,4096,256]{2,1,0:T(8,128)(2,1)} %param.14) | copy-start | bytes 6291460
  76.7 39.6 %all-to-all-start.1 = ((bf16[32,1,32]{2,1,0:T(2,128)(2,1)}), bf16[32,1,32]{2,1,0:T(2,128)(2,1)}, u32[]{:S(2)}, u32[]{:S(2)}) async-start(bf16[32,1,32]{2,1,0:T(2,128)(2,1)} %copy.161), calls=%async_computation.1 | async-start | bytes 32768 | tf_op jit(solution)/shard_map/all_to_all | solution.py:137
  114.9 60.1 %copy-start.19 = (bf16[1,64,512]{2,1,0:T(8,128)(2,1)S(1)}, bf16[1,64,512]{2,1,0:T(8,128)(2,1)}, u32[]{:S(2)}) copy-start(bf16[1,64,512]{2,1,0:T(8,128)(2,1)} %get-tuple-element.7) | copy-start | bytes 196612
  114.9 60.1 %copy-start.18 = (bf16[1,64,512]{2,1,0:T(8,128)(2,1)S(1)}, bf16[1,64,512]{2,1,0:T(8,128)(2,1)}, u32[]{:S(2)}) copy-start(bf16[1,64,512]{2,1,0:T(8,128)(2,1)} %get-tuple-element.8) | copy-start | bytes 196612
  116.3 24.2 %all-to-all-start = ((bf16[32,1,128]{2,1,0:T(2,128)(2,1)}), bf16[32,1,128]{2,1,0:T(2,128)(2,1)S(1)}, u32[]{:S(2)}, u32[]{:S(2)}) async-start(bf16[32,1,128]{2,1,0:T(2,128)(2,1)} %copy.159), calls=%async_computation | async-start | bytes 32768 | tf_op jit(solution)/shard_map/all_to_all | solution.py:136
  170.8 5.0 collective-permute-start
  208.4 17.4 %all-to-all-start.3 = ((bf16[32,1,32]{2,1,0:T(2,128)(2,1)}), bf16[32,1,32]{2,1,0:T(2,128)(2,1)S(1)}, u32[]{:S(2)}, u32[]{:S(2)}) async-start(bf16[32,1,32]{2,1,0:T(2,128)(2,1)} %copy.167), calls=%async_computation.3 | async-start | bytes 32768 | tf_op jit(solution)/shard_map/all_to_all | solution.py:137
  216.1 61.4 %copy-start.17 = (bf16[1,64,512]{2,1,0:T(8,128)(2,1)S(1)}, bf16[1,64,512]{2,1,0:T(8,128)(2,1)}, u32[]{:S(2)}) copy-start(bf16[1,64,512]{2,1,0:T(8,128)(2,1)} %get-tuple-element.9) | copy-start | bytes 196612
  216.1 61.5 %copy-start.16 = (bf16[1,64,512]{2,1,0:T(8,128)(2,1)S(1)}, bf16[1,64,512]{2,1,0:T(8,128)(2,1)}, u32[]{:S(2)}) copy-start(bf16[1,64,512]{2,1,0:T(8,128)(2,1)} %get-tuple-element.10) | copy-start | bytes 196612
  225.8 16.5 %all-to-all-start.2 = ((bf16[32,1,128]{2,1,0:T(2,128)(2,1)}), bf16[32,1,128]{2,1,0:T(2,128)(2,1)S(1)}, u32[]{:S(2)}, u32[]{:S(2)}) async-start(bf16[32,1,128]{2,1,0:T(2,128)(2,1)} %copy.165), calls=%async_computation.2 | async-start | bytes 32768 | tf_op jit(solution)/shard_map/all_to_all | solution.py:136
  272.5 5.8 collective-permute-start.1
  311.4 17.5 %all-to-all-start.5 = ((bf16[32,1,32]{2,1,0:T(2,128)(2,1)}), bf16[32,1,32]{2,1,0:T(2,128)(2,1)S(1)}, u32[]{:S(2)}, u32[]{:S(2)}) async-start(bf16[32,1,32]{2,1,0:T(2,128)(2,1)} %copy.173), calls=%async_computation.5 | async-start | bytes 32768 | tf_op jit(solution)/shard_map/all_to_all | solution.py:137
  319.2 61.7 %copy-start.15 = (bf16[1,64,512]{2,1,0:T(8,128)(2,1)S(1)}, bf16[1,64,512]{2,1,0:T(8,128)(2,1)}, u32[]{:S(2)}) copy-start(bf16[1,64,512]{2,1,0:T(8,128)(2,1)} %get-tuple-element.11) | copy-start | bytes 196612
  319.2 61.7 %copy-start.14 = (bf16[1,64,512]{2,1,0:T(8,128)(2,1)S(1)}, bf16[1,64,512]{2,1,0:T(8,128)(2,1)}, u32[]{:S(2)}) copy-start(bf16[1,64,512]{2,1,0:T(8,128)(2,1)} %get-tuple-element.12) | copy-start | bytes 196612
  328.9 16.4 %all-to-all-start.4 = ((bf16[32,1,128]{2,1,0:T(2,128)(2,1)}), bf16[32,1,128]{2,1,0:T(2,128)(2,1)S(1)}, u32[]{:S(2)}, u32[]{:S(2)}) async-start(bf16[32,1,128]{2,1,0:T(2,128)(2,1)} %copy.171), calls=%async_computation.4 | async-start | bytes 32768 | tf_op jit(solution)/shard_map/all_to_all | solution.py:136
  375.8 5.8 collective-permute-start.2
  414.1 17.5 %all-to-all-start.7 = ((bf16[32,1,32]{2,1,0:T(2,128)(2,1)}), bf16[32,1,32]{2,1,0:T(2,128)(2,1)S(1)}, u32[]{:S(2)}, u32[]{:S(2)}) async-start(bf16[32,1,32]{2,1,0:T(2,128)(2,1)} %copy.179), calls=%async_computation.7 | async-start | bytes 32768 | tf_op jit(solution)/shard_map/all_to_all | solution.py:137
  421.9 61.4 %copy-start.13 = (bf16[1,64,512]{2,1,0:T(8,128)(2,1)S(1)}, bf16[1,64,512]{2,1,0:T(8,128)(2,1)}, u32[]{:S(2)}) copy-start(bf16[1,64,512]{2,1,0:T(8,128)(2,1)} %get-tuple-element.13) | copy-start | bytes 196612
  421.9 61.4 %copy-start.12 = (bf16[1,64,512]{2,1,0:T(8,128)(2,1)S(1)}, bf16[1,64,512]{2,1,0:T(8,128)(2,1)}, u32[]{:S(2)}) copy-start(bf16[1,64,512]{2,1,0:T(8,128)(2,1)} %get-tuple-element.14) | copy-start | bytes 196612
  431.6 16.4 %all-to-all-start.6 = ((bf16[32,1,128]{2,1,0:T(2,128)(2,1)}), bf16[32,1,128]{2,1,0:T(2,128)(2,1)S(1)}, u32[]{:S(2)}, u32[]{:S(2)}) async-start(bf16[32,1,128]{2,1,0:T(2,128)(2,1)} %copy.177), calls=%async_computation.6 | async-start | bytes 32768 | tf_op jit(solution)/shard_map/all_to_all | solution.py:136
  478.3 5.8 collective-permute-start.3
  515.8 23.8 %copy-start.33 = (f32[64]{0:T(128)S(1)}, f32[64]{0:T(128)}, u32[]{:S(2)}) copy-start(f32[64]{0:T(128)} %get-tuple-element.149) | copy-start | bytes 772
  515.8 23.8 %copy-start.34 = (f32[64]{0:T(128)S(1)}, f32[64]{0:T(128)}, u32[]{:S(2)}) copy-start(f32[64]{0:T(128)} %get-tuple-element.150) | copy-start | bytes 772
  516.8 18.0 %all-to-all-start.9 = ((bf16[32,1,32]{2,1,0:T(2,128)(2,1)}), bf16[32,1,32]{2,1,0:T(2,128)(2,1)S(1)}, u32[]{:S(2)}, u32[]{:S(2)}) async-start(bf16[32,1,32]{2,1,0:T(2,128)(2,1)} %copy.185), calls=%async_computation.9 | async-start | bytes 32768 | tf_op jit(solution)/shard_map/all_to_all | solution.py:137
  524.6 62.0 %copy-start.11 = (bf16[1,64,512]{2,1,0:T(8,128)(2,1)S(1)}, bf16[1,64,512]{2,1,0:T(8,128)(2,1)}, u32[]{:S(2)}) copy-start(bf16[1,64,512]{2,1,0:T(8,128)(2,1)} %get-tuple-element.15) | copy-start | bytes 196612
  524.6 62.0 %copy-start.10 = (bf16[1,64,512]{2,1,0:T(8,128)(2,1)S(1)}, bf16[1,64,512]{2,1,0:T(8,128)(2,1)}, u32[]{:S(2)}) copy-start(bf16[1,64,512]{2,1,0:T(8,128)(2,1)} %get-tuple-element.16) | copy-start | bytes 196612
  534.8 16.4 %all-to-all-start.8 = ((bf16[32,1,128]{2,1,0:T(2,128)(2,1)}), bf16[32,1,128]{2,1,0:T(2,128)(2,1)S(1)}, u32[]{:S(2)}, u32[]{:S(2)}) async-start(bf16[32,1,128]{2,1,0:T(2,128)(2,1)} %copy.183), calls=%async_computation.8 | async-start | bytes 32768 | tf_op jit(solution)/shard_map/all_to_all | solution.py:136
  581.5 5.8 collective-permute-start.4
  619.0 23.3 %copy-start.31 = (f32[64]{0:T(128)S(1)}, f32[64]{0:T(128)}, u32[]{:S(2)}) copy-start(f32[64]{0:T(128)} %get-tuple-element.151) | copy-start | bytes 772
  619.0 23.3 %copy-start.32 = (f32[64]{0:T(128)S(1)}, f32[64]{0:T(128)}, u32[]{:S(2)}) copy-start(f32[64]{0:T(128)} %get-tuple-element.152) | copy-start | bytes 772
  619.9 17.5 %all-to-all-start.11 = ((bf16[32,1,32]{2,1,0:T(2,128)(2,1)}), bf16[32,1,32]{2,1,0:T(2,128)(2,1)S(1)}, u32[]{:S(2)}, u32[]{:S(2)}) async-start(bf16[32,1,32]{2,1,0:T(2,128)(2,1)} %copy.191), calls=%async_computation.11 | async-start | bytes 32768 | tf_op jit(solution)/shard_map/all_to_all | solution.py:137
  627.6 62.9 %copy-start.9 = (bf16[1,64,512]{2,1,0:T(8,128)(2,1)S(1)}, bf16[1,64,512]{2,1,0:T(8,128)(2,1)}, u32[]{:S(2)}) copy-start(bf16[1,64,512]{2,1,0:T(8,128)(2,1)} %get-tuple-element.17) | copy-start | bytes 196612
  627.6 62.9 %copy-start.8 = (bf16[1,64,512]{2,1,0:T(8,128)(2,1)S(1)}, bf16[1,64,512]{2,1,0:T(8,128)(2,1)}, u32[]{:S(2)}) copy-start(bf16[1,64,512]{2,1,0:T(8,128)(2,1)} %get-tuple-element.18) | copy-start | bytes 196612
  637.4 16.5 %all-to-all-start.10 = ((bf16[32,1,128]{2,1,0:T(2,128)(2,1)}), bf16[32,1,128]{2,1,0:T(2,128)(2,1)S(1)}, u32[]{:S(2)}, u32[]{:S(2)}) async-start(bf16[32,1,128]{2,1,0:T(2,128)(2,1)} %copy.189), calls=%async_computation.10 | async-start | bytes 32768 | tf_op jit(solution)/shard_map/all_to_all | solution.py:136
  684.3 7.0 collective-permute-start.5
  723.8 17.5 %all-to-all-start.13 = ((bf16[32,1,32]{2,1,0:T(2,128)(2,1)}), bf16[32,1,32]{2,1,0:T(2,128)(2,1)S(1)}, u32[]{:S(2)}, u32[]{:S(2)}) async-start(bf16[32,1,32]{2,1,0:T(2,128)(2,1)} %copy.197), calls=%async_computation.13 | async-start | bytes 32768 | tf_op jit(solution)/shard_map/all_to_all | solution.py:137
  731.6 63.0 %copy-start.7 = (bf16[1,64,512]{2,1,0:T(8,128)(2,1)S(1)}, bf16[1,64,512]{2,1,0:T(8,128)(2,1)}, u32[]{:S(2)}) copy-start(bf16[1,64,512]{2,1,0:T(8,128)(2,1)} %get-tuple-element.19) | copy-start | bytes 196612
  731.6 63.1 %copy-start.6 = (bf16[1,64,512]{2,1,0:T(8,128)(2,1)S(1)}, bf16[1,64,512]{2,1,0:T(8,128)(2,1)}, u32[]{:S(2)}) copy-start(bf16[1,64,512]{2,1,0:T(8,128)(2,1)} %get-tuple-element.20) | copy-start | bytes 196612
  741.3 16.4 %all-to-all-start.12 = ((bf16[32,1,128]{2,1,0:T(2,128)(2,1)}), bf16[32,1,128]{2,1,0:T(2,128)(2,1)S(1)}, u32[]{:S(2)}, u32[]{:S(2)}) async-start(bf16[32,1,128]{2,1,0:T(2,128)(2,1)} %copy.195), calls=%async_computation.12 | async-start | bytes 32768 | tf_op jit(solution)/shard_map/all_to_all | solution.py:136
  788.4 7.0 collective-permute-start.6
  827.9 17.4 %all-to-all-start.15 = ((bf16[32,1,32]{2,1,0:T(2,128)(2,1)}), bf16[32,1,32]{2,1,0:T(2,128)(2,1)S(1)}, u32[]{:S(2)}, u32[]{:S(2)}) async-start(bf16[32,1,32]{2,1,0:T(2,128)(2,1)} %copy.203), calls=%async_computation.15 | async-start | bytes 32768 | tf_op jit(solution)/shard_map/all_to_all | solution.py:137
  835.6 62.7 %copy-start.5 = (bf16[1,64,512]{2,1,0:T(8,128)(2,1)S(1)}, bf16[1,64,512]{2,1,0:T(8,128)(2,1)}, u32[]{:S(2)}) copy-start(bf16[1,64,512]{2,1,0:T(8,128)(2,1)} %get-tuple-element.21) | copy-start | bytes 196612
  835.6 62.7 %copy-start.4 = (bf16[1,64,512]{2,1,0:T(8,128)(2,1)S(1)}, bf16[1,64,512]{2,1,0:T(8,128)(2,1)}, u32[]{:S(2)}) copy-start(bf16[1,64,512]{2,1,0:T(8,128)(2,1)} %get-tuple-element.22) | copy-start | bytes 196612
  845.4 16.4 %all-to-all-start.14 = ((bf16[32,1,128]{2,1,0:T(2,128)(2,1)}), bf16[32,1,128]{2,1,0:T(2,128)(2,1)S(1)}, u32[]{:S(2)}, u32[]{:S(2)}) async-start(bf16[32,1,128]{2,1,0:T(2,128)(2,1)} %copy.201), calls=%async_computation.14 | async-start | bytes 32768 | tf_op jit(solution)/shard_map/all_to_all | solution.py:136
  892.1 7.0 collective-permute-start.7
  930.8 23.3 %copy-start.25 = (f32[64]{0:T(128)S(1)}, f32[64]{0:T(128)}, u32[]{:S(2)}) copy-start(f32[64]{0:T(128)} %get-tuple-element.157) | copy-start | bytes 772
  931.7 17.5 %all-to-all-start.17 = ((bf16[32,1,32]{2,1,0:T(2,128)(2,1)}), bf16[32,1,32]{2,1,0:T(2,128)(2,1)S(1)}, u32[]{:S(2)}, u32[]{:S(2)}) async-start(bf16[32,1,32]{2,1,0:T(2,128)(2,1)} %copy.209), calls=%async_computation.17 | async-start | bytes 32768 | tf_op jit(solution)/shard_map/all_to_all | solution.py:137
  949.2 16.5 %all-to-all-start.16 = ((bf16[32,1,128]{2,1,0:T(2,128)(2,1)}), bf16[32,1,128]{2,1,0:T(2,128)(2,1)S(1)}, u32[]{:S(2)}, u32[]{:S(2)}) async-start(bf16[32,1,128]{2,1,0:T(2,128)(2,1)} %copy.207), calls=%async_computation.16 | async-start | bytes 32768 | tf_op jit(solution)/shard_map/all_to_all | solution.py:136
  (23 other events, 347.9 us)
where the time goes:
time: 1030 us; the launch traced here: 1020 us
  blocking collectives  602 us (58%)
  waiting for transfers between devices  181 us (18%)
  starting transfers between devices  139 us (13%)
  matrix products  31.6 us (3%)
  other arithmetic  30 us (3%)
  local copies, waits for them, and re-layouts  29.9 us (3%)
    all_gather x18, blocking collectives, all_blocks(): tiles = lax.all_gather(tiles, axes[k], axis=0, tiled=True)  320 us
    all_gather x9, blocking collectives, shards(): lax.all_gather(mixture, TENSOR, axis=0, tiled=True)  260 us
    all_to_all x9, waiting for transfers between devices, shards(): lax.all_to_all(queries, TENSOR, split_axis=0, concat_axis=1, tiled=True)  102 us
    all_to_all x9, waiting for transfers between devices, shards(): lax.all_to_all(fresh_kv, TENSOR, split_axis=0, concat_axis=1, tiled=True)  73.3 us
    all_to_all x9, starting transfers between devices, shards(): lax.all_to_all(fresh_kv, TENSOR, split_axis=0, concat_axis=1, tiled=True)  50.8 us
    all_to_all x9, starting transfers between devices, shards(): lax.all_to_all(queries, TENSOR, split_axis=0, concat_axis=1, tiled=True)  50 us
    ppermute x8, starting transfers between devices, shifted(): lax.ppermute(value, axis, [(source, source + steps) for source in range(i...  37.8 us
    all_to_all x1, blocking collectives, shards(): lax.all_to_all(outgoing, 'section', split_axis=1, concat_axis=0, tiled=True)  22 us
  transfers between devices with their start and end apart: 26, of which 25 were waited for; matrix products, arithmetic and copies ran while one was open for 6% of the time, Pallas kernels for 0%

commit v1 on v0

--- a/solution.py
+++ b/solution.py
@@ -21,7 +21,9 @@
 def all_blocks(shard, axes, turns):
     tiles = shard[None]
     for k in turns:
-        tiles = lax.all_gather(tiles, axes[k], axis=0, tiled=True)
+        tiles = jnp.concatenate(
+            lax.all_to_all(jnp.stack([tiles] * lax.axis_size(axes[k])), axes[k], 0, 0), axis=0
+        )
     block = [lax.axis_size(axes[k]) for k in reversed(turns)]
     tiles = tiles.reshape(*block, *shard.shape)
     turned = sorted(range(len(turns)), key=lambda place: turns[len(turns) - 1 - place])

time: 1030 us -> 983 us (0.954)
  blocking collectives: 602 us -> 318 us
  waiting for transfers between devices: 181 us -> 334 us
  starting transfers between devices: 139 us -> 222 us
    all_gather x18 -> x0, blocking collectives: 320 us -> none  [all_blocks(): tiles = lax.all_gather(tiles, axes[k], axis=0, tiled=True)]
    all_to_all x0 -> x9, waiting for transfers between devices: none -> 137 us  [all_blocks(): lax.all_to_all(jnp.stack([tiles] * lax.axis_size(axes[k])), axes[k], 0, 0)]
    all_to_all x0 -> x9, starting transfers between devices: none -> 82.7 us  [all_blocks(): lax.all_to_all(jnp.stack([tiles] * lax.axis_size(axes[k])), axes[k], 0, 0)]
    all_to_all x0 -> x9, blocking collectives: none -> 37.8 us  [all_blocks(): lax.all_to_all(jnp.stack([tiles] * lax.axis_size(axes[k])), axes[k], 0, 0)]
  transfers between devices with their start and end apart: 26 -> 35, of which waited for: 25 -> 35; matrix products, arithmetic and copies ran while one was open for 6% -> 5% of each run, Pallas kernels for 0% -> 0%
where the time goes in v1:
time: 983 us; the launch traced here: 972 us
  waiting for transfers between devices  334 us (34%)
  blocking collectives  318 us (32%)
  starting transfers between devices  222 us (23%)
  matrix products  36.7 us (4%)
  local copies, waits for them, and re-layouts  30.3 us (3%)
  other arithmetic  23.2 us (2%)
    all_gather x9, blocking collectives, shards(): lax.all_gather(mixture, TENSOR, axis=0, tiled=True)  260 us
    all_to_all x9, waiting for transfers between devices, all_blocks(): lax.all_to_all(jnp.stack([tiles] * lax.axis_size(axes[k])), axes[k], 0, 0)  137 us
    all_to_all x9, waiting for transfers between devices, shards(): lax.all_to_all(queries, TENSOR, split_axis=0, concat_axis=1, tiled=True)  103 us
    all_to_all x9, starting transfers between devices, all_blocks(): lax.all_to_all(jnp.stack([tiles] * lax.axis_size(axes[k])), axes[k], 0, 0)  82.7 us
    all_to_all x9, waiting for transfers between devices, shards(): lax.all_to_all(fresh_kv, TENSOR, split_axis=0, concat_axis=1, tiled=True)  82.7 us
    all_to_all x9, starting transfers between devices, shards(): lax.all_to_all(fresh_kv, TENSOR, split_axis=0, concat_axis=1, tiled=True)  60 us
    all_to_all x9, starting transfers between devices, shards(): lax.all_to_all(queries, TENSOR, split_axis=0, concat_axis=1, tiled=True)  42.9 us
    all_to_all x9, blocking collectives, all_blocks(): lax.all_to_all(jnp.stack([tiles] * lax.axis_size(axes[k])), axes[k], 0, 0)  37.8 us
  transfers between devices with their start and end apart: 35, of which 35 were waited for; matrix products, arithmetic and copies ran while one was open for 5% of the time, Pallas kernels for 0%

profile of v1, /device:TPU:80, one launch (start us, length us, event | category | flops | bytes accessed | tf_op | source)
XLA Modules:
  0.0 971.6 jit_solution(7299557875515542564)
XLA Ops:
  1.8 43.7 %all-to-all-start = ((bf16[16,1,32,256]{3,2,1,0:T(8,128)(2,1)}), bf16[16,1,32,256]{3,2,1,0:T(8,128)(2,1)S(1)}, u32[]{:S(2)}, u32[]{:S(2)}) async-start(bf16[16,1,32,256]{3,2,1,0:T(8,128)(2,1)} %stack.54), calls=%async_computation | async-start | bytes 524288 | tf_op jit(solution)/shard_map/all_to_all | solution.py:25
  52.3 11.3 %all-to-all-done = bf16[16,1,32,256]{3,2,1,0:T(8,128)(2,1)S(1)} async-done(((bf16[16,1,32,256]{3,2,1,0:T(8,128)(2,1)}), bf16[16,1,32,256]{3,2,1,0:T(8,128)(2,1)S(1)}, u32[]{:S(2)}, u32[]{:S(2)}) %all-to-all-start) | async-done | bytes 262176 | tf_op jit(solution)/shard_map/all_to_all | solution.py:25
  69.3 6.9 all-to-all-start.3
  78.9 9.1 all-to-all-done.3
  93.1 11.4 %all-to-all-done.2 = bf16[32,1,128]{2,1,0:T(2,128)(2,1)S(1)} async-done(((bf16[32,1,128]{2,1,0:T(2,128)(2,1)}), bf16[32,1,128]{2,1,0:T(2,128)(2,1)S(1)}, u32[]{:S(2)}, u32[]{:S(2)}) %all-to-all-start.2) | async-done | bytes 8224 | tf_op jit(solution)/shard_map/all_to_all | solution.py:138
  105.5 28.9 %all-gather = bf16[32,1,4096]{2,1,0:T(2,128)(2,1)S(1)} all-gather(bf16[1,1,4096]{2,1,0:T(2,128)(2,1)S(1)} %reshape.2294), channel_id=1, replica_groups=mesh['groups'=2,'tensor_0'=16,'tensor_1'=2,'section'=8] {'tensor_0','ten..., dimensions={0}, use_global_device_ids=true | all-gather | bytes 270336 | tf_op jit(solution)/shard_map/all_gather | solution.py:156
  148.2 15.3 %all-to-all-done.4 = bf16[16,1,32,256]{3,2,1,0:T(8,128)(2,1)S(1)} async-done(((bf16[16,1,32,256]{3,2,1,0:T(8,128)(2,1)}), bf16[16,1,32,256]{3,2,1,0:T(8,128)(2,1)S(1)}, u32[]{:S(2)}, u32[]{:S(2)}) %all-to-all-start.4) | async-done | bytes 262176 | tf_op jit(solution)/shard_map/all_to_all | solution.py:25
  169.3 6.6 all-to-all-start.7
  178.6 9.1 all-to-all-done.7
  192.8 11.4 %all-to-all-done.6 = bf16[32,1,128]{2,1,0:T(2,128)(2,1)S(1)} async-done(((bf16[32,1,128]{2,1,0:T(2,128)(2,1)}), bf16[32,1,128]{2,1,0:T(2,128)(2,1)S(1)}, u32[]{:S(2)}, u32[]{:S(2)}) %all-to-all-start.6) | async-done | bytes 8224 | tf_op jit(solution)/shard_map/all_to_all | solution.py:138
  207.2 28.9 %all-gather.1 = bf16[32,1,4096]{2,1,0:T(2,128)(2,1)S(1)} all-gather(bf16[1,1,4096]{2,1,0:T(2,128)(2,1)S(1)} %reshape.2296), channel_id=1, replica_groups=mesh['groups'=2,'tensor_0'=16,'tensor_1'=2,'section'=8] {'tensor_0','ten..., dimensions={0}, use_global_device_ids=true | all-gather | bytes 270336 | tf_op jit(solution)/shard_map/all_gather | solution.py:156
  249.6 16.1 %all-to-all-done.8 = bf16[16,1,32,256]{3,2,1,0:T(8,128)(2,1)S(1)} async-done(((bf16[16,1,32,256]{3,2,1,0:T(8,128)(2,1)}), bf16[16,1,32,256]{3,2,1,0:T(8,128)(2,1)S(1)}, u32[]{:S(2)}, u32[]{:S(2)}) %all-to-all-start.8) | async-done | bytes 262176 | tf_op jit(solution)/shard_map/all_to_all | solution.py:25
  271.6 6.6 all-to-all-start.11
  280.9 9.1 all-to-all-done.11
  295.1 11.4 %all-to-all-done.10 = bf16[32,1,128]{2,1,0:T(2,128)(2,1)S(1)} async-done(((bf16[32,1,128]{2,1,0:T(2,128)(2,1)}), bf16[32,1,128]{2,1,0:T(2,128)(2,1)S(1)}, u32[]{:S(2)}, u32[]{:S(2)}) %all-to-all-start.10) | async-done | bytes 8224 | tf_op jit(solution)/shard_map/all_to_all | solution.py:138
  307.5 28.9 %all-gather.2 = bf16[32,1,4096]{2,1,0:T(2,128)(2,1)S(1)} all-gather(bf16[1,1,4096]{2,1,0:T(2,128)(2,1)S(1)} %reshape.2298), channel_id=1, replica_groups=mesh['groups'=2,'tensor_0'=16,'tensor_1'=2,'section'=8] {'tensor_0','ten..., dimensions={0}, use_global_device_ids=true | all-gather | bytes 270336 | tf_op jit(solution)/shard_map/all_gather | solution.py:156
  350.4 15.5 %all-to-all-done.12 = bf16[16,1,32,256]{3,2,1,0:T(8,128)(2,1)S(1)} async-done(((bf16[16,1,32,256]{3,2,1,0:T(8,128)(2,1)}), bf16[16,1,32,256]{3,2,1,0:T(8,128)(2,1)S(1)}, u32[]{:S(2)}, u32[]{:S(2)}) %all-to-all-start.12) | async-done | bytes 262176 | tf_op jit(solution)/shard_map/all_to_all | solution.py:25
  371.7 6.6 all-to-all-start.15
  381.0 9.1 all-to-all-done.15
  395.2 11.4 %all-to-all-done.14 = bf16[32,1,128]{2,1,0:T(2,128)(2,1)S(1)} async-done(((bf16[32,1,128]{2,1,0:T(2,128)(2,1)}), bf16[32,1,128]{2,1,0:T(2,128)(2,1)S(1)}, u32[]{:S(2)}, u32[]{:S(2)}) %all-to-all-start.14) | async-done | bytes 8224 | tf_op jit(solution)/shard_map/all_to_all | solution.py:138
  409.4 28.9 %all-gather.3 = bf16[32,1,4096]{2,1,0:T(2,128)(2,1)S(1)} all-gather(bf16[1,1,4096]{2,1,0:T(2,128)(2,1)S(1)} %reshape.2300), channel_id=1, replica_groups=mesh['groups'=2,'tensor_0'=16,'tensor_1'=2,'section'=8] {'tensor_0','ten..., dimensions={0}, use_global_device_ids=true | all-gather | bytes 270336 | tf_op jit(solution)/shard_map/all_gather | solution.py:156
  451.9 16.0 %all-to-all-done.16 = bf16[16,1,32,256]{3,2,1,0:T(8,128)(2,1)S(1)} async-done(((bf16[16,1,32,256]{3,2,1,0:T(8,128)(2,1)}), bf16[16,1,32,256]{3,2,1,0:T(8,128)(2,1)S(1)}, u32[]{:S(2)}, u32[]{:S(2)}) %all-to-all-start.16) | async-done | bytes 262176 | tf_op jit(solution)/shard_map/all_to_all | solution.py:25
  473.7 6.8 all-to-all-start.19
  483.2 9.6 all-to-all-done.19
  497.8 11.4 %all-to-all-done.18 = bf16[32,1,128]{2,1,0:T(2,128)(2,1)S(1)} async-done(((bf16[32,1,128]{2,1,0:T(2,128)(2,1)}), bf16[32,1,128]{2,1,0:T(2,128)(2,1)S(1)}, u32[]{:S(2)}, u32[]{:S(2)}) %all-to-all-start.18) | async-done | bytes 8224 | tf_op jit(solution)/shard_map/all_to_all | solution.py:138
  510.2 28.9 %all-gather.4 = bf16[32,1,4096]{2,1,0:T(2,128)(2,1)S(1)} all-gather(bf16[1,1,4096]{2,1,0:T(2,128)(2,1)S(1)} %reshape.2302), channel_id=1, replica_groups=mesh['groups'=2,'tensor_0'=16,'tensor_1'=2,'section'=8] {'tensor_0','ten..., dimensions={0}, use_global_device_ids=true | all-gather | bytes 270336 | tf_op jit(solution)/shard_map/all_gather | solution.py:156
  554.2 15.6 %all-to-all-done.20 = bf16[16,1,32,256]{3,2,1,0:T(8,128)(2,1)S(1)} async-done(((bf16[16,1,32,256]{3,2,1,0:T(8,128)(2,1)}), bf16[16,1,32,256]{3,2,1,0:T(8,128)(2,1)S(1)}, u32[]{:S(2)}, u32[]{:S(2)}) %all-to-all-start.20) | async-done | bytes 262176 | tf_op jit(solution)/shard_map/all_to_all | solution.py:25
  575.6 6.6 all-to-all-start.23
  584.9 9.1 all-to-all-done.23
  599.1 11.4 %all-to-all-done.22 = bf16[32,1,128]{2,1,0:T(2,128)(2,1)S(1)} async-done(((bf16[32,1,128]{2,1,0:T(2,128)(2,1)}), bf16[32,1,128]{2,1,0:T(2,128)(2,1)S(1)}, u32[]{:S(2)}, u32[]{:S(2)}) %all-to-all-start.22) | async-done | bytes 8224 | tf_op jit(solution)/shard_map/all_to_all | solution.py:138
  613.4 28.9 %all-gather.5 = bf16[32,1,4096]{2,1,0:T(2,128)(2,1)S(1)} all-gather(bf16[1,1,4096]{2,1,0:T(2,128)(2,1)S(1)} %reshape.2304), channel_id=1, replica_groups=mesh['groups'=2,'tensor_0'=16,'tensor_1'=2,'section'=8] {'tensor_0','ten..., dimensions={0}, use_global_device_ids=true | all-gather | bytes 270336 | tf_op jit(solution)/shard_map/all_gather | solution.py:156
  642.8 5.2 collective-permute-start.5
  657.0 16.0 %all-to-all-done.24 = bf16[16,1,32,256]{3,2,1,0:T(8,128)(2,1)S(1)} async-done(((bf16[16,1,32,256]{3,2,1,0:T(8,128)(2,1)}), bf16[16,1,32,256]{3,2,1,0:T(8,128)(2,1)S(1)}, u32[]{:S(2)}, u32[]{:S(2)}) %all-to-all-start.24) | async-done | bytes 262176 | tf_op jit(solution)/shard_map/all_to_all | solution.py:25
  678.8 6.6 all-to-all-start.27
  688.0 9.1 all-to-all-done.27
  702.3 11.4 %all-to-all-done.26 = bf16[32,1,128]{2,1,0:T(2,128)(2,1)S(1)} async-done(((bf16[32,1,128]{2,1,0:T(2,128)(2,1)}), bf16[32,1,128]{2,1,0:T(2,128)(2,1)S(1)}, u32[]{:S(2)}, u32[]{:S(2)}) %all-to-all-start.26) | async-done | bytes 8224 | tf_op jit(solution)/shard_map/all_to_all | solution.py:138
  714.7 29.3 %all-gather.6 = bf16[32,1,4096]{2,1,0:T(2,128)(2,1)S(1)} all-gather(bf16[1,1,4096]{2,1,0:T(2,128)(2,1)S(1)} %reshape.2306), channel_id=1, replica_groups=mesh['groups'=2,'tensor_0'=16,'tensor_1'=2,'section'=8] {'tensor_0','ten..., dimensions={0}, use_global_device_ids=true | all-gather | bytes 270336 | tf_op jit(solution)/shard_map/all_gather | solution.py:156
  759.3 15.4 %all-to-all-done.28 = bf16[16,1,32,256]{3,2,1,0:T(8,128)(2,1)S(1)} async-done(((bf16[16,1,32,256]{3,2,1,0:T(8,128)(2,1)}), bf16[16,1,32,256]{3,2,1,0:T(8,128)(2,1)S(1)}, u32[]{:S(2)}, u32[]{:S(2)}) %all-to-all-start.28) | async-done | bytes 262176 | tf_op jit(solution)/shard_map/all_to_all | solution.py:25
  780.5 6.6 all-to-all-start.31
  789.8 9.1 all-to-all-done.31
  804.0 11.4 %all-to-all-done.30 = bf16[32,1,128]{2,1,0:T(2,128)(2,1)S(1)} async-done(((bf16[32,1,128]{2,1,0:T(2,128)(2,1)}), bf16[32,1,128]{2,1,0:T(2,128)(2,1)S(1)}, u32[]{:S(2)}, u32[]{:S(2)}) %all-to-all-start.30) | async-done | bytes 8224 | tf_op jit(solution)/shard_map/all_to_all | solution.py:138
  818.4 28.9 %all-gather.7 = bf16[32,1,4096]{2,1,0:T(2,128)(2,1)S(1)} all-gather(bf16[1,1,4096]{2,1,0:T(2,128)(2,1)S(1)} %reshape.2308), channel_id=1, replica_groups=mesh['groups'=2,'tensor_0'=16,'tensor_1'=2,'section'=8] {'tensor_0','ten..., dimensions={0}, use_global_device_ids=true | all-gather | bytes 270336 | tf_op jit(solution)/shard_map/all_gather | solution.py:156
  861.9 16.0 %all-to-all-done.32 = bf16[16,1,32,256]{3,2,1,0:T(8,128)(2,1)S(1)} async-done(((bf16[16,1,32,256]{3,2,1,0:T(8,128)(2,1)}), bf16[16,1,32,256]{3,2,1,0:T(8,128)(2,1)S(1)}, u32[]{:S(2)}, u32[]{:S(2)}) %all-to-all-start.32) | async-done | bytes 262176 | tf_op jit(solution)/shard_map/all_to_all | solution.py:25
  883.8 6.6 all-to-all-start.35
  893.0 9.1 all-to-all-done.35
  907.3 11.4 %all-to-all-done.34 = bf16[32,1,128]{2,1,0:T(2,128)(2,1)S(1)} async-done(((bf16[32,1,128]{2,1,0:T(2,128)(2,1)}), bf16[32,1,128]{2,1,0:T(2,128)(2,1)S(1)}, u32[]{:S(2)}, u32[]{:S(2)}) %all-to-all-start.34) | async-done | bytes 8224 | tf_op jit(solution)/shard_map/all_to_all | solution.py:138
  919.7 28.9 %all-gather.8 = bf16[32,1,4096]{2,1,0:T(2,128)(2,1)S(1)} all-gather(bf16[1,1,4096]{2,1,0:T(2,128)(2,1)S(1)} %reshape.2310), channel_id=1, replica_groups=mesh['groups'=2,'tensor_0'=16,'tensor_1'=2,'section'=8] {'tensor_0','ten..., dimensions={0}, use_global_device_ids=true | all-gather | bytes 270336 | tf_op jit(solution)/shard_map/all_gather | solution.py:156
  950.6 20.3 %all_to_all.372 = bf16[8,2,1024]{2,1,0:T(2,128)(2,1)S(1)} all-to-all(bf16[8,2,1024]{2,1,0:T(2,128)(2,1)S(1)} %reshape.2355), channel_id=1, replica_groups=mesh['groups'=2,'tensor_0'=16,'tensor_1'=2,'section'=8] {'section'}, dimensions={0} | all-to-all | bytes 65536 | tf_op jit(solution)/shard_map/all_to_all | solution.py:171
  (380 shorter events, 252.2 us)
Async XLA Ops:
  0.0 134.4 %copy-start = (bf16[1,4096,256]{2,1,0:T(8,128)(2,1)S(1)}, bf16[1,4096,256]{2,1,0:T(8,128)(2,1)}, u32[]{:S(2)}) copy-start(bf16[1,4096,256]{2,1,0:T(8,128)(2,1)} %param.14) | copy-start | bytes 6291460
  0.0 52.2 %copy-start.9 = (bf16[1,128]{1,0:T(2,128)(2,1)S(1)}, bf16[1,128]{1,0:T(2,128)(2,1)}, u32[]{:S(2)}) copy-start(bf16[1,128]{1,0:T(2,128)(2,1)} %param.12) | copy-start | bytes 772
  1.8 61.8 %all-to-all-start = ((bf16[16,1,32,256]{3,2,1,0:T(8,128)(2,1)}), bf16[16,1,32,256]{3,2,1,0:T(8,128)(2,1)S(1)}, u32[]{:S(2)}, u32[]{:S(2)}) async-start(bf16[16,1,32,256]{3,2,1,0:T(8,128)(2,1)} %stack.54), calls=%async_computation | async-start | bytes 524288 | tf_op jit(solution)/shard_map/all_to_all | solution.py:25
  63.6 4.9 copy-start.1
  69.3 18.7 %all-to-all-start.3 = ((bf16[32,1,32]{2,1,0:T(2,128)(2,1)}), bf16[32,1,32]{2,1,0:T(2,128)(2,1)S(1)}, u32[]{:S(2)}, u32[]{:S(2)}) async-start(bf16[32,1,32]{2,1,0:T(2,128)(2,1)} %copy.113), calls=%async_computation.3 | async-start | bytes 32768 | tf_op jit(solution)/shard_map/all_to_all | solution.py:139
  88.0 16.5 %all-to-all-start.2 = ((bf16[32,1,128]{2,1,0:T(2,128)(2,1)}), bf16[32,1,128]{2,1,0:T(2,128)(2,1)S(1)}, u32[]{:S(2)}, u32[]{:S(2)}) async-start(bf16[32,1,128]{2,1,0:T(2,128)(2,1)} %copy.111), calls=%async_computation.2 | async-start | bytes 32768 | tf_op jit(solution)/shard_map/all_to_all | solution.py:138
  104.8 41.4 %copy-start.2 = (bf16[1,6,16,1024]{3,2,1,0:T(8,128)(2,1)S(1)}, bf16[1,6,16,1024]{3,2,1,0:T(8,128)(2,1)}, u32[]{:S(2)}) copy-start(bf16[1,6,16,1024]{3,2,1,0:T(8,128)(2,1)} %param.15) | copy-start | bytes 589828
  134.9 5.0 collective-permute-start
  140.7 22.9 %all-to-all-start.4 = ((bf16[16,1,32,256]{3,2,1,0:T(8,128)(2,1)}), bf16[16,1,32,256]{3,2,1,0:T(8,128)(2,1)S(1)}, u32[]{:S(2)}, u32[]{:S(2)}) async-start(bf16[16,1,32,256]{3,2,1,0:T(8,128)(2,1)} %stack.56), calls=%async_computation.4 | async-start | bytes 524288 | tf_op jit(solution)/shard_map/all_to_all | solution.py:25
  169.3 18.4 %all-to-all-start.7 = ((bf16[32,1,32]{2,1,0:T(2,128)(2,1)}), bf16[32,1,32]{2,1,0:T(2,128)(2,1)S(1)}, u32[]{:S(2)}, u32[]{:S(2)}) async-start(bf16[32,1,32]{2,1,0:T(2,128)(2,1)} %copy.119), calls=%async_computation.7 | async-start | bytes 32768 | tf_op jit(solution)/shard_map/all_to_all | solution.py:139
  187.8 16.5 %all-to-all-start.6 = ((bf16[32,1,128]{2,1,0:T(2,128)(2,1)}), bf16[32,1,128]{2,1,0:T(2,128)(2,1)S(1)}, u32[]{:S(2)}, u32[]{:S(2)}) async-start(bf16[32,1,128]{2,1,0:T(2,128)(2,1)} %copy.117), calls=%async_computation.6 | async-start | bytes 32768 | tf_op jit(solution)/shard_map/all_to_all | solution.py:138
  236.7 5.4 collective-permute-start.1
  242.8 22.9 %all-to-all-start.8 = ((bf16[16,1,32,256]{3,2,1,0:T(8,128)(2,1)}), bf16[16,1,32,256]{3,2,1,0:T(8,128)(2,1)S(1)}, u32[]{:S(2)}, u32[]{:S(2)}) async-start(bf16[16,1,32,256]{3,2,1,0:T(8,128)(2,1)} %stack.58), calls=%async_computation.8 | async-start | bytes 524288 | tf_op jit(solution)/shard_map/all_to_all | solution.py:25
  271.6 18.4 %all-to-all-start.11 = ((bf16[32,1,32]{2,1,0:T(2,128)(2,1)}), bf16[32,1,32]{2,1,0:T(2,128)(2,1)S(1)}, u32[]{:S(2)}, u32[]{:S(2)}) async-start(bf16[32,1,32]{2,1,0:T(2,128)(2,1)} %copy.125), calls=%async_computation.11 | async-start | bytes 32768 | tf_op jit(solution)/shard_map/all_to_all | solution.py:139
  290.0 16.5 %all-to-all-start.10 = ((bf16[32,1,128]{2,1,0:T(2,128)(2,1)}), bf16[32,1,128]{2,1,0:T(2,128)(2,1)S(1)}, u32[]{:S(2)}, u32[]{:S(2)}) async-start(bf16[32,1,128]{2,1,0:T(2,128)(2,1)} %copy.123), calls=%async_computation.10 | async-start | bytes 32768 | tf_op jit(solution)/shard_map/all_to_all | solution.py:138
  306.5 42.0 %copy-start.7 = (s32[4]{0:T(128)S(1)}, s32[4]{0:T(128)}, u32[]{:S(2)}) copy-start(s32[4]{0:T(128)} %get-tuple-element.102) | copy-start | bytes 52
  306.5 42.0 %copy-start.8 = (s32[4]{0:T(128)S(1)}, s32[4]{0:T(128)}, u32[]{:S(2)}) copy-start(s32[4]{0:T(128)} %get-tuple-element.103) | copy-start | bytes 52
  336.9 5.4 collective-permute-start.2
  343.0 22.9 %all-to-all-start.12 = ((bf16[16,1,32,256]{3,2,1,0:T(8,128)(2,1)}), bf16[16,1,32,256]{3,2,1,0:T(8,128)(2,1)S(1)}, u32[]{:S(2)}, u32[]{:S(2)}) async-start(bf16[16,1,32,256]{3,2,1,0:T(8,128)(2,1)} %stack.60), calls=%async_computation.12 | async-start | bytes 524288 | tf_op jit(solution)/shard_map/all_to_all | solution.py:25
  371.7 18.4 %all-to-all-start.15 = ((bf16[32,1,32]{2,1,0:T(2,128)(2,1)}), bf16[32,1,32]{2,1,0:T(2,128)(2,1)S(1)}, u32[]{:S(2)}, u32[]{:S(2)}) async-start(bf16[32,1,32]{2,1,0:T(2,128)(2,1)} %copy.131), calls=%async_computation.15 | async-start | bytes 32768 | tf_op jit(solution)/shard_map/all_to_all | solution.py:139
  390.1 16.5 %all-to-all-start.14 = ((bf16[32,1,128]{2,1,0:T(2,128)(2,1)}), bf16[32,1,128]{2,1,0:T(2,128)(2,1)S(1)}, u32[]{:S(2)}, u32[]{:S(2)}) async-start(bf16[32,1,128]{2,1,0:T(2,128)(2,1)} %copy.129), calls=%async_computation.14 | async-start | bytes 32768 | tf_op jit(solution)/shard_map/all_to_all | solution.py:138
  438.8 5.5 collective-permute-start.3
  445.0 22.9 %all-to-all-start.16 = ((bf16[16,1,32,256]{3,2,1,0:T(8,128)(2,1)}), bf16[16,1,32,256]{3,2,1,0:T(8,128)(2,1)S(1)}, u32[]{:S(2)}, u32[]{:S(2)}) async-start(bf16[16,1,32,256]{3,2,1,0:T(8,128)(2,1)} %stack.62), calls=%async_computation.16 | async-start | bytes 524288 | tf_op jit(solution)/shard_map/all_to_all | solution.py:25
  473.7 19.0 %all-to-all-start.19 = ((bf16[32,1,32]{2,1,0:T(2,128)(2,1)}), bf16[32,1,32]{2,1,0:T(2,128)(2,1)S(1)}, u32[]{:S(2)}, u32[]{:S(2)}) async-start(bf16[32,1,32]{2,1,0:T(2,128)(2,1)} %copy.137), calls=%async_computation.19 | async-start | bytes 32768 | tf_op jit(solution)/shard_map/all_to_all | solution.py:139
  492.7 16.5 %all-to-all-start.18 = ((bf16[32,1,128]{2,1,0:T(2,128)(2,1)}), bf16[32,1,128]{2,1,0:T(2,128)(2,1)S(1)}, u32[]{:S(2)}, u32[]{:S(2)}) async-start(bf16[32,1,128]{2,1,0:T(2,128)(2,1)} %copy.135), calls=%async_computation.18 | async-start | bytes 32768 | tf_op jit(solution)/shard_map/all_to_all | solution.py:138
  509.2 43.2 %copy-start.5 = (s32[4]{0:T(128)S(1)}, s32[4]{0:T(128)}, u32[]{:S(2)}) copy-start(s32[4]{0:T(128)} %get-tuple-element.100) | copy-start | bytes 52
  509.2 43.2 %copy-start.6 = (s32[4]{0:T(128)S(1)}, s32[4]{0:T(128)}, u32[]{:S(2)}) copy-start(s32[4]{0:T(128)} %get-tuple-element.101) | copy-start | bytes 52
  539.6 6.6 collective-permute-start.4
  547.0 22.9 %all-to-all-start.20 = ((bf16[16,1,32,256]{3,2,1,0:T(8,128)(2,1)}), bf16[16,1,32,256]{3,2,1,0:T(8,128)(2,1)S(1)}, u32[]{:S(2)}, u32[]{:S(2)}) async-start(bf16[16,1,32,256]{3,2,1,0:T(8,128)(2,1)} %stack.64), calls=%async_computation.20 | async-start | bytes 524288 | tf_op jit(solution)/shard_map/all_to_all | solution.py:25
  575.6 18.4 %all-to-all-start.23 = ((bf16[32,1,32]{2,1,0:T(2,128)(2,1)}), bf16[32,1,32]{2,1,0:T(2,128)(2,1)S(1)}, u32[]{:S(2)}, u32[]{:S(2)}) async-start(bf16[32,1,32]{2,1,0:T(2,128)(2,1)} %copy.143), calls=%async_computation.23 | async-start | bytes 32768 | tf_op jit(solution)/shard_map/all_to_all | solution.py:139
  594.0 16.5 %all-to-all-start.22 = ((bf16[32,1,128]{2,1,0:T(2,128)(2,1)}), bf16[32,1,128]{2,1,0:T(2,128)(2,1)S(1)}, u32[]{:S(2)}, u32[]{:S(2)}) async-start(bf16[32,1,128]{2,1,0:T(2,128)(2,1)} %copy.141), calls=%async_computation.22 | async-start | bytes 32768 | tf_op jit(solution)/shard_map/all_to_all | solution.py:138
  642.8 6.6 collective-permute-start.5
  650.1 22.9 %all-to-all-start.24 = ((bf16[16,1,32,256]{3,2,1,0:T(8,128)(2,1)}), bf16[16,1,32,256]{3,2,1,0:T(8,128)(2,1)S(1)}, u32[]{:S(2)}, u32[]{:S(2)}) async-start(bf16[16,1,32,256]{3,2,1,0:T(8,128)(2,1)} %stack.66), calls=%async_computation.24 | async-start | bytes 524288 | tf_op jit(solution)/shard_map/all_to_all | solution.py:25
  678.8 18.4 %all-to-all-start.27 = ((bf16[32,1,32]{2,1,0:T(2,128)(2,1)}), bf16[32,1,32]{2,1,0:T(2,128)(2,1)S(1)}, u32[]{:S(2)}, u32[]{:S(2)}) async-start(bf16[32,1,32]{2,1,0:T(2,128)(2,1)} %copy.149), calls=%async_computation.27 | async-start | bytes 32768 | tf_op jit(solution)/shard_map/all_to_all | solution.py:139
  697.2 16.5 %all-to-all-start.26 = ((bf16[32,1,128]{2,1,0:T(2,128)(2,1)}), bf16[32,1,128]{2,1,0:T(2,128)(2,1)S(1)}, u32[]{:S(2)}, u32[]{:S(2)}) async-start(bf16[32,1,128]{2,1,0:T(2,128)(2,1)} %copy.147), calls=%async_computation.26 | async-start | bytes 32768 | tf_op jit(solution)/shard_map/all_to_all | solution.py:138
  713.7 43.7 %copy-start.3 = (s32[4]{0:T(128)S(1)}, s32[4]{0:T(128)}, u32[]{:S(2)}) copy-start(s32[4]{0:T(128)} %get-tuple-element.98) | copy-start | bytes 52
  713.7 43.7 %copy-start.4 = (s32[4]{0:T(128)S(1)}, s32[4]{0:T(128)}, u32[]{:S(2)}) copy-start(s32[4]{0:T(128)} %get-tuple-element.99) | copy-start | bytes 52
  744.5 6.6 collective-permute-start.6
  751.9 22.9 %all-to-all-start.28 = ((bf16[16,1,32,256]{3,2,1,0:T(8,128)(2,1)}), bf16[16,1,32,256]{3,2,1,0:T(8,128)(2,1)S(1)}, u32[]{:S(2)}, u32[]{:S(2)}) async-start(bf16[16,1,32,256]{3,2,1,0:T(8,128)(2,1)} %stack.68), calls=%async_computation.28 | async-start | bytes 524288 | tf_op jit(solution)/shard_map/all_to_all | solution.py:25
  780.5 18.4 %all-to-all-start.31 = ((bf16[32,1,32]{2,1,0:T(2,128)(2,1)}), bf16[32,1,32]{2,1,0:T(2,128)(2,1)S(1)}, u32[]{:S(2)}, u32[]{:S(2)}) async-start(bf16[32,1,32]{2,1,0:T(2,128)(2,1)} %copy.155), calls=%async_computation.31 | async-start | bytes 32768 | tf_op jit(solution)/shard_map/all_to_all | solution.py:139
  798.9 16.5 %all-to-all-start.30 = ((bf16[32,1,128]{2,1,0:T(2,128)(2,1)}), bf16[32,1,128]{2,1,0:T(2,128)(2,1)S(1)}, u32[]{:S(2)}, u32[]{:S(2)}) async-start(bf16[32,1,128]{2,1,0:T(2,128)(2,1)} %copy.153), calls=%async_computation.30 | async-start | bytes 32768 | tf_op jit(solution)/shard_map/all_to_all | solution.py:138
  847.8 6.6 collective-permute-start.7
  855.1 22.9 %all-to-all-start.32 = ((bf16[16,1,32,256]{3,2,1,0:T(8,128)(2,1)}), bf16[16,1,32,256]{3,2,1,0:T(8,128)(2,1)S(1)}, u32[]{:S(2)}, u32[]{:S(2)}) async-start(bf16[16,1,32,256]{3,2,1,0:T(8,128)(2,1)} %stack.70), calls=%async_computation.32 | async-start | bytes 524288 | tf_op jit(solution)/shard_map/all_to_all | solution.py:25
  883.8 18.4 %all-to-all-start.35 = ((bf16[32,1,32]{2,1,0:T(2,128)(2,1)}), bf16[32,1,32]{2,1,0:T(2,128)(2,1)S(1)}, u32[]{:S(2)}, u32[]{:S(2)}) async-start(bf16[32,1,32]{2,1,0:T(2,128)(2,1)} %copy.161), calls=%async_computation.35 | async-start | bytes 32768 | tf_op jit(solution)/shard_map/all_to_all | solution.py:139
  902.2 16.5 %all-to-all-start.34 = ((bf16[32,1,128]{2,1,0:T(2,128)(2,1)}), bf16[32,1,128]{2,1,0:T(2,128)(2,1)S(1)}, u32[]{:S(2)}, u32[]{:S(2)}) async-start(bf16[32,1,128]{2,1,0:T(2,128)(2,1)} %copy.159), calls=%async_computation.34 | async-start | bytes 32768 | tf_op jit(solution)/shard_map/all_to_all | solution.py:138
